TPU v7x, 32 devices: a whole 2x2x4 slice. The times are simulated.
32 devices in a mesh: dp: 4 (over y, x), expert: 8 (over z, core).
Axes of the slice: x: 2, y: 2, z: 4, core: 2. Of those that a mesh axis runs over, the one named last changes fastest.
Arguments:
- grad_out: bfloat16 [4096, 3072], P(('dp', 'expert')), may hold values from -6 to 6
- expert_ids: int32 [4096, 2], P(('dp', 'expert')), may hold values from 0 to 7, all different within a row; in each aligned block of 128 rows (0 to 127, 128 to 255, ...) at most 36 rows name the same one
- down_weight: bfloat16 [8, 1024, 3072], P('expert'), may hold values from -0.109375 to 0.109375
- history_grad: float32 [8, 8], replicated, may hold values from 0.5 to 3
- history_hidden: float32 [8, 8], replicated, may hold values from 0.5 to 3
Outputs:
- hidden_scaled: bfloat16 [4, 8, 288, 1024], P('dp', 'expert')
- new_history_grad: float32 [8, 8], replicated
- new_history_hidden: float32 [8, 8], replicated
Inputs may be any that keep to these rules, and one draw needn't show every extreme that they name: `expert_ids`: each row names 2 different experts; among the 128 rows of one device no expert is named more than 36 times, a bound that some block reaches in some devices.
All inputs are finite; a program needn't handle non-finite values.
Results may differ from a plain program's by a relative error of at most 0.0045.
Values may be sent and summed in bfloat16 or wider, within the bound.
A program may use at most 128 MiB of HBM per device.

v0:
```python
import functools

import jax
import jax.numpy as jnp
from jax import lax
from jax.experimental import pallas as pl
from jax.experimental.pallas import tpu as pltpu
from jax.sharding import PartitionSpec as P

MESH = pl.DeviceIdType.MESH
PARTS = 4
LANES = 128
RELAYED = (3, 3)
DIRECT = (3, 3)
ORDER = ((0, 0), (1, 0), (0, 1), (1, 1), (1, 2), (1, 3))
TAKE = (3,)


def flip_bits(q, k, count):
    out, bit = 0, 1
    while bit < count:
        a, b = (q // bit) % 2, (k // bit) % 2
        out = out + bit * (a + b - 2 * a * b)
        bit *= 2
    return out


def kernel(
    n_dp, n_exp, experts, capacity,
    grad_hbm, ids_ref, hist_g_ref, hist_h_ref, weight_hbm,
    out_ref, best_ref,
    grad_ref, held, weight, send, send_rest, recv, recv_rest, rest_rows, slots, mine, peaks_in,
    grad_sem, weight_sem, send_sem, recv_sem, send_rest_sem, recv_rest_sem, peak_send_sem, peak_recv_sem,
):
    tokens = grad_ref.shape[0]
    main = send.shape[1]
    slices = n_exp // experts
    chips = n_exp // 2
    my_dp, me = lax.axis_index("dp"), lax.axis_index("expert")
    q0, c0 = me // 2, me % 2
    partner = q0 * 2 + 1 - c0
    own = me // slices
    grad_load = pltpu.make_async_copy(grad_hbm, grad_ref, grad_sem)
    grad_load.start()
    load = pltpu.make_async_copy(weight_hbm.at[0], weight, weight_sem)

    barrier = pltpu.get_barrier_semaphore()

    everyone = n_dp * n_exp
    here = my_dp * n_exp + me

    def greet(j, x):
        peer = (here + j) % everyone
        pl.semaphore_signal(
            barrier, inc=1, device_id=(peer // n_exp, peer % n_exp), device_id_type=MESH
        )
        return x

    lax.fori_loop(1, everyone, greet, 0)

    expert_row = lax.broadcasted_iota(jnp.int32, (LANES, tokens), 0)
    ids = ids_ref[...]
    mask_t = jnp.where((ids[0:1, :] == expert_row) | (ids[1:2, :] == expert_row), 1.0, 0.0)
    row = lax.broadcasted_iota(jnp.int32, (tokens, tokens), 0)
    col = lax.broadcasted_iota(jnp.int32, (tokens, tokens), 1)
    earlier = jnp.where(row < col, 1.0, 0.0).astype(jnp.bfloat16)
    before = jnp.dot(mask_t.astype(jnp.bfloat16), earlier, preferred_element_type=jnp.float32)
    slots[...] = jnp.where(mask_t > 0.5, before, -1.0)
    scale_in = 1.0 / jnp.max(hist_g_ref[...], axis=0, keepdims=True)
    scale_hidden = 1.0 / jnp.max(hist_h_ref[...], axis=0, keepdims=True)
    which = lax.broadcasted_iota(jnp.int32, (1, experts), 1)

    def pick(values, e):
        return jnp.sum(jnp.where(which == e, values, 0.0), axis=1, keepdims=True)

    position = lax.broadcasted_iota(jnp.int32, (capacity, tokens), 0).astype(jnp.float32)

    def prepare(e):
        onehot = jnp.where(slots[pl.ds(e, 1), :] == position, 1.0, 0.0).astype(jnp.bfloat16)
        rows = jnp.dot(onehot, grad_ref[...], preferred_element_type=jnp.float32)
        block = jnp.clip(rows * pick(scale_in, e), -1.0, 1.0)
        send[e] = block[0:main].astype(jnp.bfloat16)
        send_rest[e] = block[main:capacity].astype(jnp.bfloat16)

    span = weight.shape[1] // PARTS

    def outgoing(d, p):
        columns = pl.ds(p * span, span)
        return pltpu.make_async_remote_copy(
            src_ref=send.at[d // slices, :, columns], dst_ref=recv.at[me, :, columns],
            send_sem=send_sem.at[p, d], recv_sem=recv_sem.at[p, me],
            device_id=(my_dp, d), device_id_type=MESH,
        )

    def outgoing_rest(d):
        return pltpu.make_async_remote_copy(
            src_ref=send_rest.at[d // slices], dst_ref=recv_rest.at[me],
            send_sem=send_rest_sem.at[d], recv_sem=recv_rest_sem.at[me],
            device_id=(my_dp, d), device_id_type=MESH,
        )

    def incoming(s, p):
        columns = pl.ds(p * span, span)
        return pltpu.make_async_remote_copy(
            src_ref=send.at[0, :, columns], dst_ref=recv.at[s, :, columns],
            send_sem=send_sem.at[p, s], recv_sem=recv_sem.at[p, s],
            device_id=(my_dp, s), device_id_type=MESH,
        )

    def incoming_rest(s):
        return pltpu.make_async_remote_copy(
            src_ref=send_rest.at[0], dst_ref=recv_rest.at[s],
            send_sem=send_rest_sem.at[s], recv_sem=recv_rest_sem.at[s],
            device_id=(my_dp, s), device_id_type=MESH,
        )

    def chip_of(j):
        k = j
        if chips & (chips - 1) == 0:
            return flip_bits(q0, k, chips)
        return (q0 + k) % chips

    def source_of(j):
        if chips & (chips - 1) == 0:
            return chip_of(j)
        k = j
        return (q0 + chips - k) % chips

    def prepare_pair(q):
        prepare(2 * q + c0)
        prepare(2 * q + 1 - c0)

    def send_pair(q):
        for p in range(PARTS):
            for c in (c0, 1 - c0):
                outgoing(2 * q + c, p).start()
                if p == 0:
                    outgoing_rest(2 * q + c).start()

    greeted = everyone - 1
    grad_load.wait()
    load.start()
    if slices == 1:
        prepare_pair(chip_of(jnp.int32(1)))
        pl.semaphore_wait(barrier, greeted)

        def step(j, x):
            prepare_pair(chip_of((j + 1) % chips))
            send_pair(chip_of(j))
            return x
    else:
        def fill(e, x):
            prepare(e)
            return x

        lax.fori_loop(0, experts, fill, 0)
        pl.semaphore_wait(barrier, greeted)

        def step(j, x):
            send_pair(chip_of(j))
            return x

    lax.fori_loop(1, chips, step, 0)
    for p in range(PARTS):
        outgoing(partner, p).start()
    outgoing_rest(partner).start()

    recv[me] = send[own]
    recv_rest[me] = send_rest[own]
    row_peak = jnp.max(jnp.abs(grad_ref[...]).astype(jnp.float32), axis=1, keepdims=True)
    grad_peak = jnp.max(jnp.where(mask_t.T > 0.5, row_peak, 0.0), axis=0, keepdims=True)

    back = 1.0 / pick(scale_in, own)
    own_hidden = pick(scale_hidden, own)
    load.wait()

    def times_weight(block, columns):
        return lax.dot_general(
            block, weight[:, columns], (((1,), (1,)), ((), ())), preferred_element_type=jnp.float32
        )

    def multiply(block):
        return finish(times_weight(block, slice(None)))

    def finish(product):
        hidden = product * back
        scaled = jnp.clip(hidden * own_hidden, -1.0, 1.0)
        return scaled, jnp.max(jnp.max(jnp.abs(hidden), axis=0, keepdims=True), axis=1, keepdims=True)

    def pair_rows(q):
        return recv[pl.ds(2 * q, 2)].reshape(2 * main, recv.shape[2])

    def put_pair(q, scaled):
        for c in range(2):
            held[2 * q + c] = scaled[c * main:(c + 1) * main].astype(jnp.bfloat16)

    def take_own():
        for p in range(PARTS):
            incoming(partner, p).wait_recv()
        scaled, peak = multiply(pair_rows(q0))
        put_pair(q0, scaled)
        return peak

    def take(j, peak):
        q = source_of(j)
        for p in range(PARTS):
            incoming(2 * q, p).wait_recv()
            incoming(2 * q + 1, p).wait_recv()
        scaled, peak_here = multiply(pair_rows(q))
        put_pair(q, scaled)
        return jnp.maximum(peak, peak_here)

    peak = lax.fori_loop(1, chips - 1, take, take_own())

    def take_rest(j, x):
        incoming_rest((me + j) % n_exp).wait_recv()
        return x

    lax.fori_loop(1, n_exp, take_rest, 0)
    rest = capacity - main
    for s in range(n_exp):
        rest_rows[s * rest:(s + 1) * rest, :] = recv_rest[s].astype(jnp.float32)
    last = source_of(jnp.int32(chips - 1))
    product = None
    for p in range(PARTS):
        incoming(2 * last, p).wait_recv()
        incoming(2 * last + 1, p).wait_recv()
        columns = slice(p * span, (p + 1) * span)
        pair = recv[pl.ds(2 * last, 2), :, columns].reshape(2 * main, span)
        block = jnp.concatenate([pair, rest_rows[:, columns].astype(jnp.bfloat16)], axis=0)
        piece = times_weight(block, columns)
        product = piece if product is None else product + piece
    scaled, peak_here = finish(product)
    peak = jnp.maximum(peak, peak_here)

    at = lax.broadcasted_iota(jnp.int32, (1, LANES), 1)
    hidden_peak = jnp.where(at == own, peak, 0.0)
    part = lax.broadcasted_iota(jnp.int32, (8, LANES), 0)
    mine[...] = jnp.where(part == 0, grad_peak, jnp.where(part == 1, hidden_peak, 0.0))

    def peak_copy(peer, slot, j):
        return pltpu.make_async_remote_copy(
            src_ref=mine, dst_ref=peaks_in.at[slot],
            send_sem=peak_send_sem.at[j], recv_sem=peak_recv_sem.at[slot],
            device_id=(peer // n_exp, peer % n_exp), device_id_type=MESH,
        )

    def peak_start(j, x):
        peak_copy((here + j) % everyone, here, j).start()
        return x

    def peak_fold(j, best):
        peer = (here + j) % everyone
        peak_copy(peer, peer, j).wait_recv()
        return jnp.maximum(best, peaks_in[peer])

    def peak_finish(j, x):
        peak_copy((here + j) % everyone, here, j).wait_send()
        return x

    lax.fori_loop(1, everyone, peak_start, 0)
    put_pair(last, scaled)
    for s in range(n_exp):
        at_row = 2 * main + s * rest
        base = s * capacity
        out_ref[base:base + main, :] = held[s]
        out_ref[base + main:base + capacity, :] = scaled[at_row:at_row + rest].astype(jnp.bfloat16)
    best = lax.fori_loop(1, everyone, peak_fold, mine[...])
    lax.fori_loop(1, everyone, peak_finish, 0)

    best_ref[...] = best

    def drain(j, x):
        for p in range(PARTS):
            outgoing((me + j) % n_exp, p).wait_send()
        outgoing_rest((me + j) % n_exp).wait_send()
        return x

    lax.fori_loop(1, n_exp, drain, 0)


def finish_kernel(hist_g_ref, hist_h_ref, best_ref, out_ref, new_g_ref, new_h_ref, final_ref):
    final_ref[...] = out_ref[...]
    keep = hist_g_ref.shape[0] - 1
    experts = hist_g_ref.shape[1]
    new_g_ref[0:keep, :] = hist_g_ref[1:keep + 1, :]
    new_g_ref[keep:keep + 1, :] = best_ref[0:1, 0:experts]
    new_h_ref[0:keep, :] = hist_h_ref[1:keep + 1, :]
    new_h_ref[keep:keep + 1, :] = best_ref[1:2, 0:experts]


def by_blocks(grad_out, expert_ids, down_weight, history_grad, history_hidden):
    tokens, width = grad_out.shape
    experts = history_grad.shape[1]
    n_dp, n_exp = lax.axis_size("dp"), lax.axis_size("expert")
    capacity = tokens * 9 // 32
    main = (capacity - 1) // 16 * 16
    rest = capacity - main
    units = down_weight.shape[1]
    vmem = pl.BlockSpec(memory_space=pltpu.VMEM)
    dma = pltpu.SemaphoreType.DMA
    out, best = pl.pallas_call(
        functools.partial(kernel, n_dp, n_exp, experts, capacity),
        out_shape=(
            jax.ShapeDtypeStruct((n_exp * capacity, units), jnp.bfloat16),
            jax.ShapeDtypeStruct((8, LANES), jnp.float32),
        ),
        in_specs=[pl.BlockSpec(memory_space=pl.ANY), vmem, vmem, vmem, pl.BlockSpec(memory_space=pl.ANY)],
        out_specs=(vmem, vmem),
        scratch_shapes=[
            pltpu.VMEM((tokens, width), jnp.bfloat16),
            pltpu.VMEM((n_exp, main, units), jnp.bfloat16),
            pltpu.VMEM((units, width), jnp.bfloat16),
            pltpu.VMEM((experts, main, width), jnp.bfloat16),
            pltpu.VMEM((experts, rest, width), jnp.bfloat16),
            pltpu.VMEM((n_exp, main, width), jnp.bfloat16),
            pltpu.VMEM((n_exp, rest, width), jnp.bfloat16),
            pltpu.VMEM((n_exp * rest, width), jnp.float32),
            pltpu.VMEM((LANES, tokens), jnp.float32),
            pltpu.VMEM((8, LANES), jnp.float32),
            pltpu.VMEM((n_dp * n_exp, 8, LANES), jnp.float32),
            dma, dma, dma((PARTS, n_exp)), dma((PARTS, n_exp)), dma((n_exp,)), dma((n_exp,)),
            dma((n_dp * n_exp,)), dma((n_dp * n_exp,)),
        ],
        compiler_params=pltpu.CompilerParams(
            collective_id=0, has_side_effects=True, vmem_limit_bytes=60 * 1024 * 1024
        ),
    )(grad_out, expert_ids.T, history_grad, history_hidden, down_weight)
    new_g, new_h, out = pl.pallas_call(
        finish_kernel,
        out_shape=(
            jax.ShapeDtypeStruct(history_grad.shape, jnp.float32),
            jax.ShapeDtypeStruct(history_hidden.shape, jnp.float32),
            jax.ShapeDtypeStruct(out.shape, out.dtype),
        ),
        in_specs=[vmem, vmem, vmem, vmem],
        out_specs=(vmem, vmem, vmem),
    )(history_grad, history_hidden, best, out)
    return out.reshape(1, 1, n_exp * capacity, units), new_g, new_h


def chunk_edges(width):
    unit, edges = width // sum(RELAYED + DIRECT), [0]
    for pieces in RELAYED + DIRECT:
        edges.append(edges[-1] + pieces * unit)
    return edges


def relay_kernel(
    n_dp, n_exp, experts, capacity,
    grad_hbm, ids_hbm, hist_g_hbm, hist_h_hbm, weight_hbm,
    out_ref, best_ref,
    grad, ids_ref, hist_g_ref, hist_h_ref, raw, weight,
    send, send_rest, far, far_rest, relay, relay_rest, recv, recv_rest,
    counter, rest_rows, acc, slots, slots_in, onehot, mine, peaks_in,
    load_sem, known, slot_send, slot_recv, raw_send, raw_recv,
    near_send, far_send, relay_send,
    chunk_recv, peak_send, peak_recv,
):
    tokens, width = grad.shape
    main = send.shape[1]
    rest = capacity - main
    half, deep = n_exp // 2, n_exp // 4
    edges = chunk_edges(width)
    hops, chunks = len(RELAYED), len(edges) - 1
    relayed = edges[hops]
    my_dp, me = lax.axis_index("dp"), lax.axis_index("expert")
    q0, c0 = me // 2, me % 2
    side = q0 // deep
    base, far_base = side * half, (1 - side) * half
    my_i, my_k = me - base, q0 - side * deep
    inner = q0 == deep - 1 + side
    outer = jnp.logical_not(inner)
    partner = q0 * 2 + 1 - c0
    kind = jnp.where(inner, 0, 1)

    def seat_of(which):
        return half + c0 * deep + side + which - 2 * side * which

    across = 2 * (deep - side) + c0
    behind = 2 * (deep - 1 + side + jnp.where(inner, 2 * side - 1, 0)) + c0
    everyone = n_dp * n_exp
    here = my_dp * n_exp + me
    turn = me * n_dp + my_dp

    def loading(src, dst, at):
        return pltpu.make_async_copy(src, dst, load_sem.at[at])

    small = (
        loading(ids_hbm, ids_ref, 0), loading(hist_g_hbm, hist_g_ref, 1), loading(hist_h_hbm, hist_h_ref, 2)
    )
    grad_load = loading(grad_hbm, grad, 3)
    load = loading(weight_hbm.at[0], weight, 4)
    for copy in small:
        copy.start()
    grad_load.start()

    def tell(semaphore, d, dp=None):
        pl.semaphore_signal(
            semaphore, inc=1, device_id=(my_dp if dp is None else dp, d), device_id_type=MESH
        )

    barrier = pltpu.get_barrier_semaphore()

    @pl.when(inner)
    def _():
        tell(barrier, across)
        tell(barrier, behind)

    tell(barrier, partner)
    if n_dp in (2, 4):
        close = [flip_bits(my_dp, bit, n_dp) for bit in (1, 2) if bit < n_dp]
    else:
        close = [(my_dp + d) % n_dp for d in range(1, n_dp)]
    for d in close:
        tell(barrier, me, d)

    expert_row = lax.broadcasted_iota(jnp.int32, (LANES, tokens), 0)
    row = lax.broadcasted_iota(jnp.int32, (tokens, tokens), 0)
    col = lax.broadcasted_iota(jnp.int32, (tokens, tokens), 1)
    earlier = jnp.where(row < col, 1.0, 0.0).astype(jnp.bfloat16)
    for copy in small:
        copy.wait()
    ids = ids_ref[...]
    mask_t = jnp.where((ids[0:1, :] == expert_row) | (ids[1:2, :] == expert_row), 1.0, 0.0)
    before = jnp.dot(mask_t.astype(jnp.bfloat16), earlier, preferred_element_type=jnp.float32)
    slots[...] = jnp.where(mask_t > 0.5, before, -1.0)
    scale_in = 1.0 / jnp.max(hist_g_ref[...], axis=0, keepdims=True)
    scale_hidden = 1.0 / jnp.max(hist_h_ref[...], axis=0, keepdims=True)
    which = lax.broadcasted_iota(jnp.int32, (1, experts), 1)

    def pick(values, e):
        return jnp.sum(jnp.where(which == e, values, 0.0), axis=1, keepdims=True)

    position = lax.broadcasted_iota(jnp.int32, (main, tokens), 0).astype(jnp.float32)
    rest_row = lax.broadcasted_iota(jnp.int32, (half * rest, tokens), 0)
    rest_position = (rest_row % rest + main).astype(jnp.float32)
    rest_group = rest_row // rest

    def spread(at, slot_row, first):
        spare = jnp.full((half * rest, tokens), -1.0, jnp.float32)
        for i in range(half):
            named = slot_row(first + i)
            onehot[at, i * main:(i + 1) * main, :] = jnp.where(
                named == position, 1.0, 0.0
            ).astype(jnp.bfloat16)
            spare = jnp.where(rest_group == i, named, spare)
        onehot[at, half * main:half * capacity, :] = jnp.where(
            spare == rest_position, 1.0, 0.0
        ).astype(jnp.bfloat16)

    def own_row(e):
        return slots[pl.ds(e, 1), :]

    group_column = lax.broadcasted_iota(jnp.int32, (half * rest, 1), 0) // rest

    def scales_of(first):
        scales = [pick(scale_in, first + i) for i in range(half)]
        spare = jnp.zeros((half * rest, 1), jnp.float32)
        for i in range(half):
            spare = jnp.where(group_column == i, scales[i], spare)
        return scales, spare

    def fill(at, source, scales, put, put_rest):
        rows = jnp.dot(onehot[at], source, preferred_element_type=jnp.float32)
        each, spare = scales
        for i in range(half):
            put(i, jnp.clip(rows[i * main:(i + 1) * main] * each[i], -1.0, 1.0).astype(jnp.bfloat16))
        ends = jnp.clip(rows[half * main:half * capacity] * spare, -1.0, 1.0)
        for i in range(half):
            put_rest(i, ends[i * rest:(i + 1) * rest].astype(jnp.bfloat16))

    def columns_of(p, origin=0):
        return slice(edges[p] - origin, edges[p + 1] - origin)

    def remote(src, dst, send_sem, recv_sem, d):
        return pltpu.make_async_remote_copy(
            src_ref=src, dst_ref=dst, send_sem=send_sem, recv_sem=recv_sem,
            device_id=(my_dp, d), device_id_type=MESH,
        )

    def sent(ref, send_sem):
        remote(ref, ref, send_sem, send_sem, partner).wait_send()

    def came(ref, recv_sem):
        remote(ref, ref, recv_sem, recv_sem, partner).wait_recv()

    def send_raw(p):
        columns = columns_of(p)
        remote(
            grad.at[:, columns], raw.at[kind, :, columns], raw_send, raw_recv.at[kind * hops + p], across
        ).start()

    def send_slots():
        remote(
            slots.at[pl.ds(0, experts)], slots_in.at[kind], slot_send, slot_recv.at[kind], across
        ).start()

    def send_near(p):
        columns = columns_of(p)
        for j in range(1, half):
            i = (my_i + j) % half
            remote(
                send.at[i, :, columns], recv.at[my_i, :, columns], near_send, chunk_recv.at[p], base + i
            ).start()
            remote(
                send_rest.at[i, :, columns], recv_rest.at[my_i, :, columns],
                near_send, chunk_recv.at[p], base + i,
            ).start()

    outside = 2 * (1 - side)
    outside_first = ((outside + c0, outside + 1 - c0), (half - 2 - outside + c0, half - 1 - outside - c0))

    def send_far(p, targets):
        columns, at = columns_of(p), half + c0 * deep + my_k
        for i in targets:
            remote(
                far.at[i, :, columns_of(p, relayed)], recv.at[at, :, columns],
                far_send, chunk_recv.at[p], far_base + i,
            ).start()

    def send_far_rest(targets):
        columns, at = pl.ds(relayed, width - relayed), half + c0 * deep + my_k
        for i in targets:
            remote(
                far_rest.at[i], recv_rest.at[at, :, columns],
                far_send, chunk_recv.at[hops], far_base + i,
            ).start()

    def send_relay(which, p):
        columns = columns_of(p)
        for j in range(1, half):
            i = (my_i + j) % half
            remote(
                relay.at[i, which, :, columns], recv.at[seat_of(which), :, columns],
                relay_send, chunk_recv.at[p], base + i,
            ).start()
            remote(
                relay_rest.at[i, which, :, columns], recv_rest.at[seat_of(which), :, columns],
                relay_send, chunk_recv.at[p], base + i,
            ).start()

    def wait_chunk(p, senders):
        size = edges[p + 1] - edges[p]
        blocks = senders * size // rest * capacity
        if p == hops:
            blocks += 2 * (width - relayed - size)
        elif p > hops:
            blocks -= 2 * size
        came(counter.at[:, 0:blocks], chunk_recv.at[p])

    spread(0, own_row, base)
    spread(1, own_row, far_base)
    near_scales = scales_of(base)
    grad_load.wait()
    load.start()
    pl.semaphore_wait(barrier, 2 + len(close))
    tell(known.at[0], partner)

    @pl.when(inner)
    def _():
        tell(known.at[0], across)
        send_slots()

        for p in range(hops):
            send_raw(p)
        pl.semaphore_wait(known.at[0], 3)
        tell(known.at[1], across)
        tell(known.at[1], behind)

    @pl.when(outer)
    def _():
        tell(known.at[0], behind)
        pl.semaphore_wait(known.at[0], 1)

    for d in close:
        tell(known.at[2], me, d)

    def direct(p):
        columns = columns_of(p)

        def put(i, block):
            send[i, :, columns] = block

        def put_rest(i, block):
            send_rest[i, :, columns] = block

        fill(0, grad[:, columns], near_scales, put, put_rest)
        send_near(p)

        if p == 1:
            pl.semaphore_wait(known.at[1], 1)
            if close:
                pl.semaphore_wait(known.at[2], len(close))

            @pl.when(outer)
            def _():
                send_slots()

        @pl.when(outer)
        def _():
            if p > 0:
                send_raw(p - 1)
            if p == chunks - 1:
                send_raw(p)

    for p in range(chunks):
        direct(p)

    def fill_far(p):
        columns = columns_of(p, relayed)

        def put(i, block):
            far[i, :, columns] = block

        def put_rest(i, block):
            far_rest[i, :, columns] = block

        fill(1, grad[:, columns_of(p)], far_scales, put, put_rest)

    far_scales = scales_of(far_base)

    @pl.when(inner)
    def _():
        for p in range(hops, chunks):
            fill_far(p)
        for targets in outside_first:
            send_far_rest(targets)
            for p in range(hops, chunks):
                send_far(p, targets)

    recv[my_i] = send[my_i]
    recv_rest[my_i] = send_rest[my_i]
    row_peak = jnp.max(jnp.abs(grad[...]).astype(jnp.float32), axis=1, keepdims=True)
    grad_peak = jnp.max(jnp.where(mask_t.T > 0.5, row_peak, 0.0), axis=0, keepdims=True)
    back = 1.0 / pick(scale_in, me)
    own_hidden = pick(scale_hidden, me)

    load.wait()

    def add_product(p, first=False):
        columns, size = columns_of(p), edges[p + 1] - edges[p]
        for s in range(n_exp):
            rest_rows[s * rest:(s + 1) * rest, 0:size] = recv_rest[s, :, columns].astype(jnp.float32)
        block = jnp.concatenate(
            [
                recv[:, :, columns].reshape(n_exp * main, size),
                rest_rows[:, 0:size].astype(jnp.bfloat16),
            ],
            axis=0,
        )
        product = lax.dot_general(
            block, weight[:, columns], (((1,), (1,)), ((), ())), preferred_element_type=jnp.float32
        )
        acc[...] = product if first else acc[...] + product

    def get_ready(which):
        @pl.when(inner)
        def _():
            came(slots_in.at[which], slot_recv.at[which])
            spread(2 + which, lambda e: slots_in[which, pl.ds(e, 1), :], base)

    def pass_on(which, p):
        columns = columns_of(p)

        @pl.when(inner)
        def _():
            came(raw.at[which, :, columns], raw_recv.at[which * hops + p])

            def put(i, block):
                relay[i, which, :, columns] = block

            def put_rest(i, block):
                relay_rest[i, which, :, columns] = block

            fill(2 + which, raw[which, :, columns], near_scales, put, put_rest)
            send_relay(which, p)
            recv[seat_of(which), :, columns] = relay[my_i, which, :, columns]
            recv_rest[seat_of(which), :, columns] = relay_rest[my_i, which, :, columns]

    def multiply(p):
        @pl.when(inner)
        def _():
            wait_chunk(p, half - 1 + deep if p < hops else n_exp - 2)

        @pl.when(outer)
        def _():
            wait_chunk(p, n_exp - 1)

        add_product(p, p == 0)

    for at, (which, p) in enumerate(ORDER):
        if p == 0:
            get_ready(which)
        pass_on(which, p)
        for taken, place in enumerate(TAKE):
            if place == at:
                multiply(taken)
    for p in range(len(TAKE), chunks):
        multiply(p)
    hidden = acc[...] * back
    peak = jnp.max(jnp.max(jnp.abs(hidden), axis=0, keepdims=True), axis=1, keepdims=True)
    lane = lax.broadcasted_iota(jnp.int32, (1, LANES), 1)
    mine[...] = jnp.where(lane < experts, grad_peak, jnp.where(lane == experts + me, peak, 0.0))
    for j in range(everyone - 1):
        peer = jnp.where(j >= turn, j + 1, j)
        pltpu.make_async_remote_copy(
            src_ref=mine, dst_ref=peaks_in.at[here], send_sem=peak_send, recv_sem=peak_recv,
            device_id=(peer % n_dp, peer // n_dp), device_id_type=MESH,
        ).start()
    peaks_in[here] = mine[...]
    scaled = jnp.clip(acc[...] * back * own_hidden, -1.0, 1.0)
    for at in range(n_exp):
        if at < half:
            block, first = side, at * capacity
        else:
            block, first = 1 - side, ((at - half) % deep * 2 + (at - half) // deep) * capacity
        out_ref[block, first:first + main, :] = scaled[at * main:(at + 1) * main].astype(jnp.bfloat16)
        tail = n_exp * main + at * rest
        out_ref[block, first + main:first + capacity, :] = scaled[tail:tail + rest].astype(jnp.bfloat16)

    per_block = capacity // rest
    sent(slots.at[pl.ds(0, experts)], slot_send)
    sent(counter.at[:, 0:(half - 1) * per_block * width], near_send)

    @pl.when(outer)
    def _():
        sent(grad, raw_send)

    @pl.when(inner)
    def _():
        sent(grad.at[:, pl.ds(0, relayed)], raw_send)
        sent(counter.at[:, 0:half * per_block * (width - relayed)], far_send)
        sent(counter.at[:, 0:(half - 1) * per_block * (relayed + width)], relay_send)

    others = peaks_in.at[pl.ds(0, everyone - 1)]
    sent(others, peak_send)
    came(others, peak_recv)
    best_ref[...] = jnp.max(peaks_in[...], axis=0)


def relay_finish(
    hist_g_ref, hist_h_ref, best_ref, out_ref, new_g_hbm, new_h_hbm, final_hbm, new_g, new_h, sem
):
    result = pltpu.make_async_copy(out_ref, final_hbm, sem.at[0])
    result.start()
    keep = hist_g_ref.shape[0] - 1
    experts = hist_g_ref.shape[1]
    new_g[0:keep, :] = hist_g_ref[1:keep + 1, :]
    new_g[keep:keep + 1, :] = best_ref[0:1, 0:experts]
    new_h[0:keep, :] = hist_h_ref[1:keep + 1, :]
    new_h[keep:keep + 1, :] = best_ref[0:1, experts:2 * experts]
    first = pltpu.make_async_copy(new_g, new_g_hbm, sem.at[1])
    second = pltpu.make_async_copy(new_h, new_h_hbm, sem.at[2])
    first.start()
    second.start()
    first.wait()
    second.wait()
    result.wait()


def by_relay(grad_out, expert_ids, down_weight, history_grad, history_hidden):
    tokens, width = grad_out.shape
    experts = history_grad.shape[1]
    n_dp, n_exp = lax.axis_size("dp"), lax.axis_size("expert")
    capacity = tokens * 9 // 32
    main = (capacity - 1) // 16 * 16
    rest = capacity - main
    units = down_weight.shape[1]
    half, deep = n_exp // 2, n_exp // 4
    edges = chunk_edges(width)
    chunks, hops = len(edges) - 1, len(RELAYED)
    span = max(after - before for before, after in zip(edges, edges[1:]))
    tail = width - edges[hops]
    everyone = n_dp * n_exp
    vmem, anywhere = pl.BlockSpec(memory_space=pltpu.VMEM), pl.BlockSpec(memory_space=pl.ANY)
    dma = pltpu.SemaphoreType.DMA
    bf16, f32 = jnp.bfloat16, jnp.float32
    out, best = pl.pallas_call(
        functools.partial(relay_kernel, n_dp, n_exp, experts, capacity),
        out_shape=(pltpu.VMEM((2, half * capacity, units), bf16), pltpu.VMEM((1, LANES), f32)),
        in_specs=[anywhere] * 5,
        out_specs=(vmem, vmem),
        scratch_shapes=[
            pltpu.VMEM((tokens, width), bf16),
            pltpu.VMEM(expert_ids.shape[::-1], jnp.int32),
            pltpu.VMEM(history_grad.shape, f32),
            pltpu.VMEM(history_hidden.shape, f32),
            pltpu.VMEM((deep, tokens, width), bf16),
            pltpu.VMEM((units, width), bf16),
            pltpu.VMEM((half, main, width), bf16),
            pltpu.VMEM((half, rest, width), bf16),
            pltpu.VMEM((half, main, tail), bf16),
            pltpu.VMEM((half, rest, tail), bf16),
            pltpu.VMEM((half, deep, main, width), bf16),
            pltpu.VMEM((half, deep, rest, width), bf16),
            pltpu.VMEM((n_exp, main, width), bf16),
            pltpu.VMEM((n_exp, rest, width), bf16),
            pltpu.VMEM((rest, 2 * half * capacity // rest * width), bf16),
            pltpu.VMEM((n_exp * rest, span), f32),
            pltpu.VMEM((n_exp * capacity, units), f32),
            pltpu.VMEM((LANES, tokens), f32),
            pltpu.VMEM((deep, experts, tokens), f32),
            pltpu.VMEM((2 + deep, half * capacity, tokens), bf16),
            pltpu.VMEM((1, LANES), f32),
            pltpu.VMEM((everyone, 1, LANES), f32),
            dma((5,)), pltpu.SemaphoreType.REGULAR((3,)), dma, dma((deep,)), dma, dma((hops + chunks,)),
            dma, dma, dma,
            dma((chunks,)), dma, dma,
        ],
        compiler_params=pltpu.CompilerParams(
            collective_id=1, has_side_effects=True, vmem_limit_bytes=56 * 1024 * 1024
        ),
    )(grad_out, expert_ids.T, history_grad, history_hidden, down_weight)
    new_g, new_h, out = pl.pallas_call(
        relay_finish,
        out_shape=(
            jax.ShapeDtypeStruct(history_grad.shape, f32),
            jax.ShapeDtypeStruct(history_hidden.shape, f32),
            jax.ShapeDtypeStruct((2, half * capacity, units), bf16),
        ),
        in_specs=[vmem, vmem, vmem, vmem],
        out_specs=(anywhere, anywhere, anywhere),
        scratch_shapes=[
            pltpu.VMEM(history_grad.shape, f32), pltpu.VMEM(history_hidden.shape, f32), dma((3,))
        ],
        compiler_params=pltpu.CompilerParams(vmem_limit_bytes=4 * 1024 * 1024),
    )(history_grad, history_hidden, best, out)
    return out.reshape(1, 1, n_exp * capacity, units), new_g, new_h


def fits_relay(tokens, width, experts, n_exp):
    capacity = tokens * 9 // 32
    return (
        experts == n_exp and n_exp // 4 == 2 and experts % 8 == 0 and 2 * experts <= LANES
        and tokens % LANES == 0 and width % (sum(RELAYED + DIRECT) * LANES) == 0
        and (n_exp // 2 * capacity) % 16 == 0 and (n_exp // 2 * (capacity % 16)) % 16 == 0
        and 0 < capacity % 16 and capacity % (capacity % 16) == 0
    )


def per_device(*arguments):
    (tokens, width), experts = arguments[0].shape, arguments[3].shape[1]
    if fits_relay(tokens, width, experts, lax.axis_size("expert")):
        return by_relay(*arguments)
    return by_blocks(*arguments)


def solution(mesh):
    in_specs = (
        P(("dp", "expert"), None),
        P(("dp", "expert"), None),
        P("expert", None, None),
        P(),
        P(),
    )
    out_specs = (P("dp", "expert", None, None), P(), P())
    return jax.shard_map(
        per_device, mesh=mesh, in_specs=in_specs, out_specs=out_specs, check_vma=False
    )
```

profile of v0, /device:TPU:0, one launch (start us, length us, event | category | flops | bytes accessed | tf_op | source)
XLA Modules:
  0.0 47.0 jit_solution(1462655183665020865)
XLA Ops:
  0.6 0.0 copy-start.1
  0.6 0.0 copy-start
  0.7 45.4 %shard_map.76 = (bf16[2,144,1024]{2,1,0:T(8,128)(2,1)S(1)}, f32[1,128]{1,0:T(1,128)S(1)}) custom-call(bf16[128,3072]{1,0:T(8,128)(2,1)} %grad_hbm.1, s32[2,128]{1,0:T(2,128)} %bitcast.2, f32[8,8]{1,0:T(8,128)} %hist_g_ref.1, f32[8,8]{1,0:T(8,128)} %hist_h_ref.1, bf16[1,1024,3072]{2,1,0:T(8,128)(2,1)} %weight_hbm.1), custom_call_target="tpu_custom_call" | custom-call | tf_op jit(solution)/shard_map/pallas_call | solution.py:779
  46.1 0.0 copy-done.1
  46.1 0.0 copy-done
  46.1 0.8 %shard_map.77 = (f32[8,8]{1,0:T(8,128)}, f32[8,8]{1,0:T(8,128)}, bf16[2,144,1024]{2,1,0:T(8,128)(2,1)}) custom-call(f32[8,8]{1,0:T(8,128)S(1)} %copy-done, f32[8,8]{1,0:T(8,128)S(1)} %copy-done.1, f32[1,128]{1,0:T(1,128)S(1)} %get-tuple-element.8.best_ref, bf16[2,144,1024]{2,1,0:T(8,128)(2,1)S(1)} %get-tuple-element.9.out_ref), custom_call_target="tpu_custom_call" | custom-call | tf_op jit(solution)/shard_map/pallas_call | solution.py:815
Async XLA Ops:
  0.6 45.5 %copy-start.1 = (f32[8,8]{1,0:T(8,128)S(1)}, f32[8,8]{1,0:T(8,128)}, u32[]{:S(2)}) copy-start(f32[8,8]{1,0:T(8,128)} %hist_h_ref.1) | copy-start | bytes 772
  0.6 45.5 %copy-start = (f32[8,8]{1,0:T(8,128)S(1)}, f32[8,8]{1,0:T(8,128)}, u32[]{:S(2)}) copy-start(f32[8,8]{1,0:T(8,128)} %hist_g_ref.1) | copy-start | bytes 772
where the time goes:
time: 47.1 us; the launch traced here: 47 us
  Pallas kernels  46.3 us (98%)
  between operations  0.67 us (1%)
    pallas_call x1, Pallas kernels, by_relay(): pl.pallas_call(functools.partial(relay_kernel, n_dp, n_exp, experts, capa...  45.4 us

commit v1 on v0

--- a/solution.py
+++ b/solution.py
@@ -10,9 +10,9 @@
 MESH = pl.DeviceIdType.MESH
 PARTS = 4
 LANES = 128
-RELAYED = (3, 3)
-DIRECT = (3, 3)
-ORDER = ((0, 0), (1, 0), (0, 1), (1, 1), (1, 2), (1, 3))
+RELAYED = (3, 3, 1)
+DIRECT = (3, 2)
+ORDER = ((0, 0), (1, 0), (0, 1), (1, 1), (1, 2), (1, 3), (0, 2), (1, 4))
 TAKE = (3,)
 
 
@@ -586,9 +586,7 @@
             send_rest[i, :, columns] = block
 
         fill(0, grad[:, columns], near_scales, put, put_rest)
-        send_near(p)
-
-        if p == 1:
+        if p == 0:
             pl.semaphore_wait(known.at[1], 1)
             if close:
                 pl.semaphore_wait(known.at[2], len(close))
@@ -596,12 +594,13 @@
             @pl.when(outer)
             def _():
                 send_slots()
-
-        @pl.when(outer)
-        def _():
-            if p > 0:
-                send_raw(p - 1)
-            if p == chunks - 1:
+                send_raw(0)
+
+        send_near(p)
+        if p > 0:
+
+            @pl.when(outer)
+            def _():
                 send_raw(p)
 
     for p in range(chunks):

time: 47.1 us -> 47 us (level)
  no operation moved by 1% of the time
where the time goes in v1:
time: 47 us; the launch traced here: 46.8 us
  Pallas kernels  46.1 us (98%)
  between operations  0.67 us (1%)
    pallas_call x1, Pallas kernels, by_relay(): pl.pallas_call(functools.partial(relay_kernel, n_dp, n_exp, experts, capa...  45.3 us

profile of v1, /device:TPU:0, one launch (start us, length us, event | category | flops | bytes accessed | tf_op | source)
XLA Modules:
  0.0 46.8 jit_solution(1573170652786040724)
XLA Ops:
  0.6 0.0 copy-start.1
  0.6 0.0 copy-start
  0.7 45.3 %shard_map.76 = (bf16[2,144,1024]{2,1,0:T(8,128)(2,1)S(1)}, f32[1,128]{1,0:T(1,128)S(1)}) custom-call(bf16[128,3072]{1,0:T(8,128)(2,1)} %grad_hbm.1, s32[2,128]{1,0:T(2,128)} %bitcast.2, f32[8,8]{1,0:T(8,128)} %hist_g_ref.1, f32[8,8]{1,0:T(8,128)} %hist_h_ref.1, bf16[1,1024,3072]{2,1,0:T(8,128)(2,1)} %weight_hbm.1), custom_call_target="tpu_custom_call" | custom-call | tf_op jit(solution)/shard_map/pallas_call | solution.py:778
  46.0 0.0 copy-done.1
  46.0 0.0 copy-done
  46.0 0.8 %shard_map.77 = (f32[8,8]{1,0:T(8,128)}, f32[8,8]{1,0:T(8,128)}, bf16[2,144,1024]{2,1,0:T(8,128)(2,1)}) custom-call(f32[8,8]{1,0:T(8,128)S(1)} %copy-done, f32[8,8]{1,0:T(8,128)S(1)} %copy-done.1, f32[1,128]{1,0:T(1,128)S(1)} %get-tuple-element.8.best_ref, bf16[2,144,1024]{2,1,0:T(8,128)(2,1)S(1)} %get-tuple-element.9.out_ref), custom_call_target="tpu_custom_call" | custom-call | tf_op jit(solution)/shard_map/pallas_call | solution.py:814
Async XLA Ops:
  0.6 45.3 %copy-start.1 = (f32[8,8]{1,0:T(8,128)S(1)}, f32[8,8]{1,0:T(8,128)}, u32[]{:S(2)}) copy-start(f32[8,8]{1,0:T(8,128)} %hist_h_ref.1) | copy-start | bytes 772
  0.6 45.3 %copy-start = (f32[8,8]{1,0:T(8,128)S(1)}, f32[8,8]{1,0:T(8,128)}, u32[]{:S(2)}) copy-start(f32[8,8]{1,0:T(8,128)} %hist_g_ref.1) | copy-start | bytes 772

commit v2 on v1

--- a/solution.py
+++ b/solution.py
@@ -10,9 +10,9 @@
 MESH = pl.DeviceIdType.MESH
 PARTS = 4
 LANES = 128
-RELAYED = (3, 3, 1)
-DIRECT = (3, 2)
-ORDER = ((0, 0), (1, 0), (0, 1), (1, 1), (1, 2), (1, 3), (0, 2), (1, 4))
+RELAYED = (3, 3)
+DIRECT = (3, 2, 1)
+ORDER = ((0, 0), (1, 0), (0, 1), (1, 1), (1, 2), (1, 3), (1, 4))
 TAKE = (3,)
 
 
@@ -511,12 +511,13 @@
     outside = 2 * (1 - side)
     outside_first = ((outside + c0, outside + 1 - c0), (half - 2 - outside + c0, half - 1 - outside - c0))
 
-    def send_far(p, targets):
-        columns, at = columns_of(p), half + c0 * deep + my_k
+    def send_far(first, after, targets):
+        at = half + c0 * deep + my_k
         for i in targets:
             remote(
-                far.at[i, :, columns_of(p, relayed)], recv.at[at, :, columns],
-                far_send, chunk_recv.at[p], far_base + i,
+                far.at[i, :, pl.ds(edges[first] - relayed, edges[after] - edges[first])],
+                recv.at[at, :, pl.ds(edges[first], edges[after] - edges[first])],
+                far_send, chunk_recv.at[first], far_base + i,
             ).start()
 
     def send_far_rest(targets):
@@ -540,13 +541,13 @@
                 relay_send, chunk_recv.at[p], base + i,
             ).start()
 
-    def wait_chunk(p, senders):
+    def wait_chunk(p, senders, ahead):
         size = edges[p + 1] - edges[p]
         blocks = senders * size // rest * capacity
         if p == hops:
-            blocks += 2 * (width - relayed - size)
+            blocks += 2 * (width - relayed - size) // rest * ahead
         elif p > hops:
-            blocks -= 2 * size
+            blocks -= 2 * size // rest * ahead
         came(counter.at[:, 0:blocks], chunk_recv.at[p])
 
     spread(0, own_row, base)
@@ -625,8 +626,9 @@
             fill_far(p)
         for targets in outside_first:
             send_far_rest(targets)
-            for p in range(hops, chunks):
-                send_far(p, targets)
+        send_far(hops, chunks, outside_first[0])
+        for p in range(hops, chunks):
+            send_far(p, p + 1, outside_first[1])
 
     recv[my_i] = send[my_i]
     recv_rest[my_i] = send_rest[my_i]
@@ -680,11 +682,11 @@
     def multiply(p):
         @pl.when(inner)
         def _():
-            wait_chunk(p, half - 1 + deep if p < hops else n_exp - 2)
+            wait_chunk(p, half - 1 + deep if p < hops else n_exp - 2, rest)
 
         @pl.when(outer)
         def _():
-            wait_chunk(p, n_exp - 1)
+            wait_chunk(p, n_exp - 1, capacity)
 
         add_product(p, p == 0)
 

time: 47 us -> 47.1 us (level)
  no operation moved by 1% of the time
where the time goes in v2:
time: 47.1 us; the launch traced here: 47 us
  Pallas kernels  46.3 us (98%)
  between operations  0.67 us (1%)
    pallas_call x1, Pallas kernels, by_relay(): pl.pallas_call(functools.partial(relay_kernel, n_dp, n_exp, experts, capa...  45.4 us

profile of v2, /device:TPU:0, one launch (start us, length us, event | category | flops | bytes accessed | tf_op | source)
XLA Modules:
  0.0 47.0 jit_solution(11756613169621996463)
XLA Ops:
  0.6 0.0 copy-start.1
  0.6 0.0 copy-start
  0.7 45.4 %shard_map.76 = (bf16[2,144,1024]{2,1,0:T(8,128)(2,1)S(1)}, f32[1,128]{1,0:T(1,128)S(1)}) custom-call(bf16[128,3072]{1,0:T(8,128)(2,1)} %grad_hbm.1, s32[2,128]{1,0:T(2,128)} %bitcast.2, f32[8,8]{1,0:T(8,128)} %hist_g_ref.1, f32[8,8]{1,0:T(8,128)} %hist_h_ref.1, bf16[1,1024,3072]{2,1,0:T(8,128)(2,1)} %weight_hbm.1), custom_call_target="tpu_custom_call" | custom-call | tf_op jit(solution)/shard_map/pallas_call | solution.py:780
  46.1 0.0 copy-done.1
  46.1 0.0 copy-done
  46.1 0.8 %shard_map.77 = (f32[8,8]{1,0:T(8,128)}, f32[8,8]{1,0:T(8,128)}, bf16[2,144,1024]{2,1,0:T(8,128)(2,1)}) custom-call(f32[8,8]{1,0:T(8,128)S(1)} %copy-done, f32[8,8]{1,0:T(8,128)S(1)} %copy-done.1, f32[1,128]{1,0:T(1,128)S(1)} %get-tuple-element.8.best_ref, bf16[2,144,1024]{2,1,0:T(8,128)(2,1)S(1)} %get-tuple-element.9.out_ref), custom_call_target="tpu_custom_call" | custom-call | tf_op jit(solution)/shard_map/pallas_call | solution.py:816
Async XLA Ops:
  0.6 45.5 %copy-start.1 = (f32[8,8]{1,0:T(8,128)S(1)}, f32[8,8]{1,0:T(8,128)}, u32[]{:S(2)}) copy-start(f32[8,8]{1,0:T(8,128)} %hist_h_ref.1) | copy-start | bytes 772
  0.6 45.5 %copy-start = (f32[8,8]{1,0:T(8,128)S(1)}, f32[8,8]{1,0:T(8,128)}, u32[]{:S(2)}) copy-start(f32[8,8]{1,0:T(8,128)} %hist_g_ref.1) | copy-start | bytes 772
